TPU v7x, 32 devices: a whole 2x2x4 slice. The times are simulated.
32 devices in a mesh: section: 4 (over z), dp: 8 (over y, x, core).
Axes of the slice: x: 2, y: 2, z: 4, core: 2. Of those that a mesh axis runs over, the one named last changes fastest.
Arguments:
- inputs: bfloat16 [2048, 2048], P('dp'), may hold values from -6 to 6
- order: int32 [8, 2], P('dp'), may hold values from 0 to 1, each once within a row
- image_start: int32 [8, 2], P('dp'), may hold values from 0 to 112, as said below
- image_len: int32 [8, 2], P('dp'), may hold values from 16 to 64
- norm_gain: float32 [4, 2048], P('section'), may hold values from 0.25 to 1.75
- qkv_weight: bfloat16 [4, 2048, 6144], P('section', 'dp'), may hold values from -0.125 to 0.125
- q_gain: float32 [4, 2048], P('section'), may hold values from 0.5 to 2.5
- k_gain: float32 [4, 2048], P('section'), may hold values from 0.5 to 2.5
- o_weight: bfloat16 [4, 2048, 2048], P('section'), may hold values from -0.125 to 0.125
Outputs:
- section_outputs: bfloat16 [4, 2048, 2048], P('section', 'dp')
Inputs may be any that keep to these rules, and one draw needn't show every extreme that they name: `order`: each row is a permutation of the micro-batch numbers. image_start + image_len <= 128 for every micro-batch.
All inputs are finite; a program needn't handle non-finite values.
Results may differ from a plain program's by a relative error of at most 0.035.
Values may be sent and summed in bfloat16 or wider, within the bound.
A program may use at most 128 MiB of HBM per device.

v0:
```python
import functools
import jax
import jax.numpy as jnp
from jax import lax
from jax.experimental import pallas as pl
from jax.experimental.pallas import tpu as pltpu
from jax.sharding import PartitionSpec as P

HEAD_DIM = 128
EPS = 1e-05
LOG2_E = 1.4426950408889634
SUBS = 2
CHUNKS = 4
WIDE = 1
EARLY_WIDE = 3
HEADS_AT_ONCE = 16
NORMS_AT_ONCE = 16
MESH = pl.DeviceIdType.MESH


def ring_order(chips):
    columns = 1
    while columns * columns < chips:
        columns *= 2
    rows = chips // columns
    cells = []
    for r in range(rows):
        line = list(range(1, columns))
        cells += [r * columns + c for c in (line if r % 2 == 0 else line[::-1])]
    cells += [r * columns for r in reversed(range(rows))]
    return cells


def look(table, index):
    found = jnp.int32(0)
    for i, value in enumerate(table):
        found = found + jnp.where(index == i, jnp.int32(value), jnp.int32(0))
    return found


def kernel(
    sections, devices,
    order_ref, start_ref, len_ref, x_ref, gain_ref, w_ref, qg_ref, kg_ref, o_ref,
    out_ref,
    wbuf, obuf, xin, xout, acc, qkv, att, early,
    own_sem, o_sem, first_send, first_recv, ring_send, ring_recv, pair_send, pair_recv,
    hop_send, hop_recv,
):
    chips = devices // 2
    order = ring_order(chips)
    inverse = [order.index(c) for c in range(chips)]
    shard = w_ref.shape[0]
    piece = shard // (2 * SUBS)
    micro, chunks, seq, width = xin.shape
    model = chunks * width
    sec = lax.axis_index("section")
    me = lax.axis_index("dp")
    core = lax.rem(me, 2)
    place = look(inverse, me // 2)
    partner = me + 1 - 2 * core

    def at(offset):
        return look(order, lax.rem(place + (offset % chips), chips)) * 2 + core

    ahead, behind = at(1), at(-1)
    above = lax.rem(sec + 1, sections)
    below = lax.rem(sec + sections - 1, sections)

    barrier = pltpu.get_barrier_semaphore()
    for other in ((sec, ahead), (sec, behind), (sec, partner), (above, me), (below, me)):
        pl.semaphore_signal(barrier, inc=1, device_id=other, device_id_type=MESH)
    pl.semaphore_wait(barrier, 5)

    own_rows = pl.ds(pl.multiple_of(me * shard, shard), shard)

    def rows(owner, way, sub):
        return pl.ds(pl.multiple_of(owner * shard + (way * SUBS + sub) * piece, piece), piece)

    def ring_copy(way, sub, step):
        owner = at(-step if way == 0 else step)
        where = rows(owner, way, sub)
        if step == 0:
            source = w_ref.at[pl.ds((way * SUBS + sub) * piece, piece)]
        else:
            source = wbuf.at[where]
        return pltpu.make_async_remote_copy(
            src_ref=source, dst_ref=wbuf.at[where],
            send_sem=ring_send.at[way, sub, step], recv_sem=ring_recv.at[way, sub, step],
            device_id=(sec, ahead if way == 0 else behind), device_id_type=MESH,
        )

    def pair_copy(way, sub, step):
        owner = at(-step if way == 0 else step)
        where = rows(owner, way, sub)
        return pltpu.make_async_remote_copy(
            src_ref=wbuf.at[where], dst_ref=wbuf.at[where],
            send_sem=pair_send.at[way, sub, step - 1], recv_sem=pair_recv.at[way, sub, step - 1],
            device_id=(sec, partner), device_id_type=MESH,
        )

    ring = {}
    pair = {}
    for sub in range(SUBS):
        for way in range(2):
            ring[way, sub, 0] = ring_copy(way, sub, 0)
            ring[way, sub, 0].start()
    first = pltpu.make_async_remote_copy(
        src_ref=w_ref, dst_ref=wbuf.at[own_rows], send_sem=first_send, recv_sem=first_recv,
        device_id=(sec, partner), device_id_type=MESH,
    )
    first.start()
    own = pltpu.make_async_copy(w_ref, wbuf.at[own_rows], own_sem)
    own.start()
    o_copy = pltpu.make_async_copy(o_ref, obuf, o_sem)
    o_copy.start()
    total = w_ref.shape[1]
    half = shard // 2

    @pl.when(sec == 0)
    def _():
        for j in range(micro):
            for n in range(model // half):
                part = x_ref[order_ref[0, j], :, n * half : (n + 1) * half].astype(jnp.float32)
                early[n, j * seq : (j + 1) * seq] = (
                    part * gain_ref[:, n * half : (n + 1) * half]
                ).astype(jnp.bfloat16)

    def absorb(halves, fresh=False):
        @pl.when(sec == 0)
        def _():
            @pl.loop(0, EARLY_WIDE)
            def _(n):
                cols = pl.ds(pl.multiple_of(n * (total // EARLY_WIDE), total // EARLY_WIDE), total // EARLY_WIDE)
                left = [early[h] for h in halves]
                right = [wbuf[pl.ds(pl.multiple_of(h * half, half), half), cols] for h in halves]
                if half % 128 == 0:
                    left = [jnp.concatenate(left, axis=1)]
                    right = [jnp.concatenate(right, axis=0)]
                for i, (one, other) in enumerate(zip(left, right)):
                    part = jnp.dot(one, other, preferred_element_type=jnp.float32)
                    if fresh and i == 0:
                        acc[:, cols] = part
                    else:
                        acc[:, cols] += part

    def mate(owner):
        return owner + 1 - 2 * core

    own.wait()
    first.wait_recv()
    absorb([2 * me, 2 * me + 1], fresh=True)
    absorb([2 * partner, 2 * partner + 1])
    for step in range(1, chips):
        for sub in range(SUBS):
            for way in range(2):
                ring[way, sub, step - 1].wait_recv()
                if step < chips - 1:
                    ring[way, sub, step] = ring_copy(way, sub, step)
                    ring[way, sub, step].start()
                pair[way, sub, step] = pair_copy(way, sub, step)
                pair[way, sub, step].start()
        for way in range(2):
            for sub in range(SUBS):
                pair[way, sub, step].wait_recv()
            owner = at(-step if way == 0 else step)
            absorb([2 * owner + way, 2 * mate(owner) + way])
    o_copy.wait()
    first.wait_send()
    for step in range(1, chips):
        for sub in range(SUBS):
            for way in range(2):
                pair[way, sub, step].wait_send()
                ring[way, sub, step - 1].wait_send()

    def hop(j, c):
        return pltpu.make_async_remote_copy(
            src_ref=xout.at[j, c], dst_ref=xin.at[j, c],
            send_sem=hop_send.at[j, c], recv_sem=hop_recv.at[j, c],
            device_id=(above, me), device_id_type=MESH,
        )

    row_id = lax.broadcasted_iota(jnp.int32, (seq, seq), 0)
    col_id = lax.broadcasted_iota(jnp.int32, (seq, seq), 1)

    @pl.loop(0, micro)
    def _(j):
        which = order_ref[0, j]
        s0 = start_ref[0, which]
        s1 = s0 + len_ref[0, which]

        own_seq = pl.ds(pl.multiple_of(j * seq, seq), seq)
        square = jnp.zeros((seq, 1), jnp.float32)
        for c in range(chunks):
            span = slice(c * width, (c + 1) * width)

            @pl.when(sec == 0)
            def _():
                xin[j, c] = x_ref[which, :, span]

            @pl.when(sec > 0)
            def _():
                hop(j, c).wait_recv()

            wide = xin[j, c].astype(jnp.float32)
            square = square + jnp.sum(wide * wide, axis=-1, keepdims=True)
            scaled = (wide * gain_ref[:, span]).astype(jnp.bfloat16)

            @pl.when(sec > 0)
            def _():
                @pl.loop(0, WIDE)
                def _(n):
                    cols = pl.ds(pl.multiple_of(n * (total // WIDE), total // WIDE), total // WIDE)
                    part = jnp.dot(scaled, wbuf[span, cols], preferred_element_type=jnp.float32)
                    if c == 0:
                        acc[own_seq, cols] = part
                    else:
                        acc[own_seq, cols] += part

        scale = lax.rsqrt(square * (1.0 / model) + EPS)

        for part, gains in ((0, qg_ref), (1, kg_ref)):
            factor = HEAD_DIM ** (-0.5) * LOG2_E if part == 0 else 1.0

            @pl.loop(0, model // (NORMS_AT_ONCE * HEAD_DIM))
            def _(n):
                for i in range(NORMS_AT_ONCE):
                    base = (n * NORMS_AT_ONCE + i) * HEAD_DIM
                    here = pl.ds(pl.multiple_of(base, HEAD_DIM), HEAD_DIM)
                    cols = pl.ds(pl.multiple_of(part * model + base, HEAD_DIM), HEAD_DIM)
                    p = acc[own_seq, cols]
                    mean = jnp.mean(p * p, axis=-1, keepdims=True) * scale * scale
                    lift = lax.rsqrt(mean + EPS) * scale
                    qkv[:, cols] = (p * lift * (gains[:, here] * factor)).astype(jnp.bfloat16)

        allowed = (col_id <= row_id) | (
            (row_id >= s0) & (row_id < s1) & (col_id >= s0) & (col_id < s1)
        )

        @pl.loop(0, model // (HEADS_AT_ONCE * HEAD_DIM))
        def _(n):
            for i in range(HEADS_AT_ONCE):
                base = (n * HEADS_AT_ONCE + i) * HEAD_DIM
                here = pl.ds(pl.multiple_of(base, HEAD_DIM), HEAD_DIM)
                q = qkv[:, here]
                k = qkv[:, pl.ds(pl.multiple_of(model + base, HEAD_DIM), HEAD_DIM)]
                v = acc[own_seq, pl.ds(pl.multiple_of(2 * model + base, HEAD_DIM), HEAD_DIM)] * scale
                scores = lax.dot_general(
                    q, k, (((1,), (1,)), ((), ())), preferred_element_type=jnp.float32
                )
                lifted = jnp.where(allowed, jnp.exp2(scores), 0.0)
                mixed = jnp.dot(
                    lifted.astype(jnp.bfloat16), v.astype(jnp.bfloat16),
                    preferred_element_type=jnp.float32,
                )
                share = 1.0 / jnp.sum(lifted, axis=-1, keepdims=True)
                att[:, here] = (mixed * share).astype(jnp.bfloat16)

        for c in range(chunks):
            span = slice(c * width, (c + 1) * width)
            grown = jnp.dot(att[...], obuf[:, span], preferred_element_type=jnp.float32)
            fresh = (xin[j, c].astype(jnp.float32) + grown).astype(jnp.bfloat16)
            xout[j, c] = fresh
            out_ref[j, :, span] = fresh

            @pl.when(sec < sections - 1)
            def _():
                hop(j, c).start()

    @pl.when(sec < sections - 1)
    def _():
        for j in range(micro):
            for c in range(chunks):
                hop(j, c).wait_send()


def solution(mesh):
    sections, devices = mesh.shape["section"], mesh.shape["dp"]

    def body(inputs, order, image_start, image_len, norm_gain, qkv_weight, q_gain, k_gain, o_weight):
        micro = order.shape[1]
        count, model = inputs.shape
        seq = count // micro
        total = qkv_weight.shape[2]
        shard = qkv_weight.shape[1]
        width = model // CHUNKS
        chunks = model // width
        chips = devices // 2
        smem = pl.BlockSpec(memory_space=pltpu.SMEM)
        vmem = pl.BlockSpec(memory_space=pltpu.VMEM)
        hbm = pl.BlockSpec(memory_space=pltpu.HBM)
        dma = pltpu.SemaphoreType.DMA
        out = pl.pallas_call(
            functools.partial(kernel, sections, devices),
            out_shape=jax.ShapeDtypeStruct((micro, seq, model), jnp.bfloat16),
            in_specs=[smem, smem, smem, vmem, vmem, hbm, vmem, vmem, hbm],
            out_specs=vmem,
            scratch_shapes=[
                pltpu.VMEM((model, total), jnp.bfloat16),
                pltpu.VMEM((model, model), jnp.bfloat16),
                pltpu.VMEM((micro, chunks, seq, width), jnp.bfloat16),
                pltpu.VMEM((micro, chunks, seq, width), jnp.bfloat16),
                pltpu.VMEM((count, total), jnp.float32),
                pltpu.VMEM((seq, 2 * model), jnp.bfloat16),
                pltpu.VMEM((seq, model), jnp.bfloat16),
                pltpu.VMEM((2 * model // shard, count, shard // 2), jnp.bfloat16),
                dma, dma, dma, dma,
                dma((2, SUBS, chips - 1)),
                dma((2, SUBS, chips - 1)),
                dma((2, SUBS, chips - 1)),
                dma((2, SUBS, chips - 1)),
                dma((micro, chunks)),
                dma((micro, chunks)),
            ],
            compiler_params=pltpu.CompilerParams(
                collective_id=0, has_side_effects=True, vmem_limit_bytes=60 * 1024 * 1024
            ),
        )(
            order, image_start, image_len, inputs.reshape(micro, seq, model), norm_gain,
            qkv_weight.reshape(shard, total), q_gain, k_gain, o_weight.reshape(model, model),
        )
        return out.reshape(1, count, model)

    in_specs = (
        P("dp", None),
        P("dp", None),
        P("dp", None),
        P("dp", None),
        P("section", None),
        P("section", "dp", None),
        P("section", None),
        P("section", None),
        P("section", None, None),
    )
    out_specs = P("section", "dp", None)
    return jax.shard_map(body, mesh=mesh, in_specs=in_specs, out_specs=out_specs, check_vma=False)
```

profile of v0, /device:TPU:24, one launch (start us, length us, event | category | flops | bytes accessed | tf_op | source)
XLA Modules:
  0.0 183.1 jit_solution(8575920020630544142)
XLA Ops:
  0.0 180.8 %shard_map.91 = bf16[2,128,2048]{2,1,0:T(8,128)(2,1)} custom-call(s32[1,2]{1,0:T(1,128)} %order_ref.1, s32[1,2]{1,0:T(1,128)} %start_ref.1, s32[1,2]{1,0:T(1,128)} %len_ref.1, bf16[2,128,2048]{2,1,0:T(8,128)(2,1)} %bitcast.7, f32[1,2048]{1,0:T(1,128)} %gain_ref.1, bf16[256,6144]{1,0:T(8,128)(2,1)} %bitcast.6, f32[1,2048]{1,0:T(1,128)} %qg_ref.1, ...), custom_call_target="tpu_custom_call" | custom-call | tf_op jit(solution)/shard_map/pallas_call | solution.py:292
  180.8 2.3 %copy.11 = bf16[1,256,2048]{2,1,0:T(8,128)(2,1)} copy(bf16[1,256,2048]{2,1,0:T(8,128)(2,1)} %bitcast.5) | data formatting | bytes 2097152
where the time goes:
time: 183 us
  Pallas kernels  181 us (99%)
  local copies, waits for them, and re-layouts  2.3 us (1%)
    pallas_call x1, Pallas kernels, body(): pl.pallas_call(functools.partial(kernel, sections, devices), out_shape=ja...  181 us

commit v1 on v0

v1 whole, which is shorter than its diff:
```python
import functools
import jax
import jax.numpy as jnp
from jax import lax
from jax.experimental import pallas as pl
from jax.experimental.pallas import tpu as pltpu
from jax.sharding import PartitionSpec as P

HEAD_DIM = 128
EPS = 1e-05
LOG2_E = 1.4426950408889634
SUBS = 2
CHUNKS = 4
WIDE = 1
HEADS_AT_ONCE = 16
NORMS_AT_ONCE = 16
SHARED_SECTIONS = 2
PARTS = 3
MESH = pl.DeviceIdType.MESH


def grid_of(chips):
    columns = 1
    while columns * columns < chips:
        columns *= 2
    return chips // columns, columns


def ring_order(chips):
    rows, columns = grid_of(chips)
    cells = []
    for r in range(rows):
        line = list(range(1, columns))
        cells += [r * columns + c for c in (line if r % 2 == 0 else line[::-1])]
    cells += [r * columns for r in reversed(range(rows))]
    return cells


def look(table, index):
    found = jnp.int32(0)
    for i, value in enumerate(table):
        found = found + jnp.where(index == i, jnp.int32(value), jnp.int32(0))
    return found


def flip(value):
    return value + 1 - 2 * lax.rem(value, 2)


def aligned(start, size):
    return pl.ds(start if isinstance(start, int) else pl.multiple_of(start, size), size)


def kernel(
    sections, devices,
    order_ref, start_ref, len_ref, x_ref, gain_ref, w_ref, qg_ref, kg_ref, o_ref,
    out_ref,
    wbuf, obuf, xin, xout, acc, qkv, att, xmate, ret, ssq, spans, mate_spans,
    own_sem, o_sem, first_send, first_recv, ring_send, ring_recv, pair_send, pair_recv,
    hop_send, hop_recv,
    own_sems, swap_send, swap_recv, loop_send, loop_recv, core_send, core_recv,
    mine_send, mine_recv, x_send, x_recv, give_send, give_recv, span_send, span_recv,
):
    chips = devices // 2
    grid_rows, columns = grid_of(chips)
    order = ring_order(chips)
    inverse = [order.index(c) for c in range(chips)]
    shard, total = w_ref.shape
    piece = shard // (2 * SUBS)
    micro, chunks, seq, width = xin.shape
    model = chunks * width
    quarter = model // 4
    few = quarter // HEAD_DIM
    sec = lax.axis_index("section")
    me = lax.axis_index("dp")
    core = lax.rem(me, 2)
    chip = lax.div(me, 2)
    place = look(inverse, chip)
    partner = flip(me)

    def at(offset):
        return look(order, lax.rem(place + (offset % chips), chips)) * 2 + core

    ahead, behind = at(1), at(-1)
    above = lax.rem(sec + 1, sections)
    below = lax.rem(sec + sections - 1, sections)

    row, col = lax.div(chip, columns), lax.rem(chip, columns)
    across, down = lax.rem(col, 2), lax.rem(row, 2)
    units = (across, 2 + down)
    half_c, half_r = columns // 2, grid_rows // 2
    places = (row * half_c + lax.div(col, 2), col * half_r + lax.div(row, 2))
    length = chips // 2

    def device(r, c):
        return (r * columns + c) * 2 + core

    mates = (device(row, flip(col)), device(flip(row), col))

    def seat(s, offset, mate):
        spot = lax.rem(places[s] + (offset % length), length)
        if s == 0:
            r, c = lax.div(spot, half_c), 2 * lax.rem(spot, half_c) + across
            c = flip(c) if mate else c
        else:
            c, r = lax.div(spot, half_r), 2 * lax.rem(spot, half_r) + down
            r = flip(r) if mate else r
        return device(r, c)

    def block(owner):
        return aligned(owner * shard, shard)

    def cols_of(unit, part):
        return aligned(part * model + unit * quarter, quarter)

    shared = sec < SHARED_SECTIONS

    def stay(s, p):
        where = cols_of(units[s], p)
        return pltpu.make_async_copy(w_ref.at[:, where], wbuf.at[block(me), where], own_sems.at[s, p])

    o_copy = pltpu.make_async_copy(o_ref, obuf, o_sem)
    own_rows = block(me)
    own = pltpu.make_async_copy(w_ref, wbuf.at[own_rows], own_sem)

    @pl.when(shared)
    def _():
        for s in range(2):
            for p in range(PARTS):
                stay(s, p).start()
        for j in range(micro):
            which = order_ref[0, j]
            s0 = start_ref[0, which]
            spans[j, 0] = jnp.full(spans.shape[2:], s0, jnp.int32)
            spans[j, 1] = jnp.full(spans.shape[2:], s0 + len_ref[0, which], jnp.int32)

            @pl.when(sec == 0)
            def _():
                for c in range(chunks):
                    xin[j, c] = x_ref[which, :, c * width : (c + 1) * width]

    @pl.when(jnp.logical_not(shared))
    def _():
        own.start()

    o_copy.start()

    barrier = pltpu.get_barrier_semaphore()
    near = [mates[0], mates[1], partner]
    if chips > 4:
        near += [ahead, behind]
        for s in range(2):
            near += [seat(s, 1, False), seat(s, -1, False)]
    for other in near:
        pl.semaphore_signal(barrier, inc=1, device_id=(sec, other), device_id_type=MESH)

    @pl.when(sec < sections - 1)
    def _():
        pl.semaphore_signal(barrier, inc=1, device_id=(above, me), device_id_type=MESH)

    @pl.when(sec > 0)
    def _():
        pl.semaphore_signal(barrier, inc=1, device_id=(below, me), device_id_type=MESH)

    line = (sec > 0).astype(jnp.int32) + (sec < sections - 1).astype(jnp.int32)
    pl.semaphore_wait(barrier, len(near) + line)

    def hop(j, c):
        return pltpu.make_async_remote_copy(
            src_ref=xout.at[j, c], dst_ref=xin.at[j, c],
            send_sem=hop_send.at[j, c], recv_sem=hop_recv.at[j, c],
            device_id=(above, me), device_id_type=MESH,
        )

    row_id = lax.broadcasted_iota(jnp.int32, (seq, seq), 0)
    col_id = lax.broadcasted_iota(jnp.int32, (seq, seq), 1)

    def mask(s0, s1):
        return (col_id <= row_id) | (
            (row_id >= s0) & (row_id < s1) & (col_id >= s0) & (col_id < s1)
        )

    def leave(j):
        for c in range(chunks):
            span = slice(c * width, (c + 1) * width)
            grown = jnp.dot(att[j], obuf[:, span], preferred_element_type=jnp.float32)
            fresh = (xin[j, c].astype(jnp.float32) + grown).astype(jnp.bfloat16)
            xout[j, c] = fresh
            out_ref[j, :, span] = fresh

            @pl.when(sec < sections - 1)
            def _():
                hop(j, c).start()

    def head(q, k, v, allowed):
        scores = lax.dot_general(
            q, k, (((1,), (1,)), ((), ())), preferred_element_type=jnp.float32
        )
        lifted = jnp.where(allowed, jnp.exp2(scores), 0.0)
        mixed = jnp.dot(
            lifted.astype(jnp.bfloat16), v.astype(jnp.bfloat16),
            preferred_element_type=jnp.float32,
        )
        return (mixed * (1.0 / jnp.sum(lifted, axis=-1, keepdims=True))).astype(jnp.bfloat16)

    def lifted_norm(p, scale, gain):
        mean = jnp.mean(p * p, axis=-1, keepdims=True) * scale * scale
        return (p * (lax.rsqrt(mean + EPS) * scale) * gain).astype(jnp.bfloat16)

    @pl.when(shared)
    def _():
        def remote(source, dest, sent, got, other):
            return pltpu.make_async_remote_copy(
                src_ref=source, dst_ref=dest, send_sem=sent, recv_sem=got,
                device_id=(sec, other), device_id_type=MESH,
            )

        def swap(s, p):
            where = cols_of(flip(units[s]), p)
            return remote(
                w_ref.at[:, where], wbuf.at[own_rows, where],
                swap_send.at[s, p], swap_recv.at[s, p], mates[s],
            )

        def circle(s, k, b, p):
            where = cols_of(units[s], p)
            rows = block(seat(s, 1 - k, b == 1))
            source = w_ref.at[:, where] if k == 1 and b == 0 else wbuf.at[rows, where]
            return remote(
                source, wbuf.at[rows, where],
                loop_send.at[s, k - 1, b, p], loop_recv.at[s, k - 1, b, p], seat(s, 1, False),
            )

        def owner_of(s, i):
            return mates[s] if i == 0 else seat(s, -((i + 1) // 2), i % 2 == 0)

        def hand(s, i, p):
            here = wbuf.at[block(owner_of(s, i)), cols_of(units[s], p)]
            return remote(here, here, core_send.at[s, i, p], core_recv.at[s, i, p], partner)

        def mine(s, p):
            where = cols_of(units[s], p)
            return remote(
                w_ref.at[:, where], wbuf.at[own_rows, where],
                mine_send.at[s, p], mine_recv.at[s, p], partner,
            )

        def share(s, j, c):
            return remote(
                xin.at[j, c], xmate.at[s, j, c], x_send.at[s, j, c], x_recv.at[s, j, c], mates[s]
            )

        def give(s, j):
            return remote(
                ret.at[s, j], att.at[j, :, aligned(units[s] * quarter, quarter)],
                give_send.at[s, j], give_recv.at[s, j], mates[s],
            )

        def tell(s):
            return remote(spans, mate_spans.at[s], span_send.at[s], span_recv.at[s], mates[s])

        both = [(p, s) for p in range(PARTS) for s in range(2)]
        waves = 2 * length - 1

        for s in range(2):
            tell(s).start()

        @pl.when(sec == 0)
        def _():
            for c in range(chunks):
                for s in range(2):
                    share(s, 0, c).start()

        for p, s in both:
            swap(s, p).start()
        for p, s in both:
            mine(s, p).start()
        for p, s in both:
            circle(s, 1, 0, p).start()

        def fold(x):
            out = x[:, :128]
            for i in range(1, x.shape[1] // 128):
                out = out + x[:, i * 128 : (i + 1) * 128]
            return out

        def take(ref, j, start, size):
            if isinstance(start, int):
                return ref[j, start // width, :, start % width : start % width + size]
            if size == width:
                return ref[j, lax.div(start, width)]
            return ref[j, lax.div(start, width), :, aligned(lax.rem(start, width), size)]

        def project(j, s, start, size, parts, fresh):
            here = aligned(start, size)
            gain = gain_ref[:, here]
            ours = take(xin, j, start, size).astype(jnp.float32)
            theirs = take(xmate.at[s], j, start, size).astype(jnp.float32)
            left = jnp.concatenate(
                [(ours * gain).astype(jnp.bfloat16), (theirs * gain).astype(jnp.bfloat16)], axis=0
            )
            for p in parts:
                cols = cols_of(units[s], p)
                part = jnp.dot(left, wbuf[here, cols], preferred_element_type=jnp.float32)
                if fresh:
                    acc[:, cols] = part
                else:
                    acc[:, cols] += part
            if 0 in parts:
                squares = [(1 + s, theirs)] + ([(0, ours)] if s == 0 else [])
                for k, x in squares:
                    if fresh:
                        ssq[k] = fold(x * x)
                    else:
                        ssq[k] += fold(x * x)

        chip_rows = 2 * shard

        @pl.when(sec == 0)
        def _():
            for c in range(chunks):
                for s in range(2):
                    share(s, 0, c).wait_recv()

        for p, s in both:
            stay(s, p).wait()
            mine(s, p).wait_recv()

        @pl.when(sec == 0)
        def _():
            for s in range(2):
                project(0, s, chip * chip_rows, chip_rows, range(PARTS), True)

        for i in range(waves):
            def finish(p):
                for s in range(2):
                    hand(s, i, p).wait_recv()

                @pl.when(sec == 0)
                def _():
                    for s in range(2):
                        start = lax.div(owner_of(s, i), 2) * chip_rows
                        project(0, s, start, chip_rows, (p,), False)

            for p in range(PARTS):
                for s in range(2):
                    if i == 0:
                        swap(s, p).wait_recv()
                        circle(s, 1, 1, p).start()
                    else:
                        k, b = (i + 1) // 2, (i + 1) % 2
                        circle(s, k, b, p).wait_recv()
                        if k < length - 1:
                            circle(s, k + 1, b, p).start()
                    hand(s, i, p).start()
                if p > 0:
                    finish(p - 1)
            finish(PARTS - 1)

        for s in range(2):
            tell(s).wait_recv()
        o_copy.wait()

        def attend(turn, region, unit, scale, allowed, ref, base):
            rows = slice(region * seq, (region + 1) * seq)
            for part, gains in ((0, qg_ref), (1, kg_ref)):
                factor = HEAD_DIM ** (-0.5) * LOG2_E if part == 0 else 1.0
                for i in range(few):
                    start = unit * quarter + i * HEAD_DIM
                    p = acc[rows, aligned(part * model + start, HEAD_DIM)]
                    spot = (turn * 2 + part) * quarter + i * HEAD_DIM
                    qkv[:, spot : spot + HEAD_DIM] = lifted_norm(
                        p, scale, gains[:, aligned(start, HEAD_DIM)] * factor
                    )
            for i in range(few):
                spot = turn * 2 * quarter + i * HEAD_DIM
                v = acc[rows, aligned(2 * model + unit * quarter + i * HEAD_DIM, HEAD_DIM)] * scale
                ref[:, aligned(base + i * HEAD_DIM, HEAD_DIM)] = head(
                    qkv[:, spot : spot + HEAD_DIM],
                    qkv[:, spot + quarter : spot + quarter + HEAD_DIM], v, allowed,
                )

        @pl.loop(0, micro)
        def _(j):
            @pl.when((sec > 0) | (j > 0))
            def _():
                def finish(c):
                    for s in range(2):
                        share(s, j, c).wait_recv()
                    for s in range(2):
                        project(j, s, c * width, width, range(PARTS), c == 0)

                for c in range(chunks):
                    @pl.when(sec > 0)
                    def _():
                        hop(j, c).wait_recv()
                        for s in range(2):
                            share(s, j, c).start()

                    if c > 0:
                        finish(c - 1)
                finish(chunks - 1)

            def scale_of(k):
                square = jnp.sum(ssq[k], axis=-1, keepdims=True)
                return lax.rsqrt(square * (1.0 / model) + EPS)

            for s in range(2):
                allowed = mask(mate_spans[s, j, 0, 0:1, :], mate_spans[s, j, 1, 0:1, :])
                attend(s, 1, units[s], scale_of(1 + s), allowed, ret.at[s, j], 0)
                give(s, j).start()

            @pl.when((sec == 0) & (j < micro - 1))
            def _():
                for c in range(chunks):
                    for s in range(2):
                        share(s, j + 1, c).start()

            which = order_ref[0, j]
            s0 = start_ref[0, which]
            allowed = mask(s0, s0 + len_ref[0, which])
            scale = scale_of(0)
            for s in range(2):
                attend(2 + s, 0, units[s], scale, allowed, att.at[j], units[s] * quarter)
            for s in range(2):
                give(s, j).wait_recv()
            leave(j)

        for s in range(2):
            tell(s).wait_send()
            for p in range(PARTS):
                swap(s, p).wait_send()
                mine(s, p).wait_send()
                for i in range(waves):
                    hand(s, i, p).wait_send()
                for k in range(1, length):
                    for b in range(2):
                        circle(s, k, b, p).wait_send()
            for j in range(micro):
                give(s, j).wait_send()
                for c in range(chunks):
                    share(s, j, c).wait_send()

    @pl.when(jnp.logical_not(shared))
    def _():
        def rows(owner, way, sub):
            return pl.ds(pl.multiple_of(owner * shard + (way * SUBS + sub) * piece, piece), piece)

        def ring_copy(way, sub, step):
            owner = at(-step if way == 0 else step)
            where = rows(owner, way, sub)
            if step == 0:
                source = w_ref.at[pl.ds((way * SUBS + sub) * piece, piece)]
            else:
                source = wbuf.at[where]
            return pltpu.make_async_remote_copy(
                src_ref=source, dst_ref=wbuf.at[where],
                send_sem=ring_send.at[way, sub, step], recv_sem=ring_recv.at[way, sub, step],
                device_id=(sec, ahead if way == 0 else behind), device_id_type=MESH,
            )

        def pair_copy(way, sub, step):
            owner = at(-step if way == 0 else step)
            where = rows(owner, way, sub)
            return pltpu.make_async_remote_copy(
                src_ref=wbuf.at[where], dst_ref=wbuf.at[where],
                send_sem=pair_send.at[way, sub, step - 1], recv_sem=pair_recv.at[way, sub, step - 1],
                device_id=(sec, partner), device_id_type=MESH,
            )

        ring = {}
        pair = {}
        for sub in range(SUBS):
            for way in range(2):
                ring[way, sub, 0] = ring_copy(way, sub, 0)
                ring[way, sub, 0].start()
        first = pltpu.make_async_remote_copy(
            src_ref=w_ref, dst_ref=wbuf.at[own_rows], send_sem=first_send, recv_sem=first_recv,
            device_id=(sec, partner), device_id_type=MESH,
        )
        first.start()
        own.wait()
        first.wait_recv()
        for step in range(1, chips):
            for sub in range(SUBS):
                for way in range(2):
                    ring[way, sub, step - 1].wait_recv()
                    if step < chips - 1:
                        ring[way, sub, step] = ring_copy(way, sub, step)
                        ring[way, sub, step].start()
                    pair[way, sub, step] = pair_copy(way, sub, step)
                    pair[way, sub, step].start()
            for way in range(2):
                for sub in range(SUBS):
                    pair[way, sub, step].wait_recv()
        o_copy.wait()
        first.wait_send()
        for step in range(1, chips):
            for sub in range(SUBS):
                for way in range(2):
                    pair[way, sub, step].wait_send()
                    ring[way, sub, step - 1].wait_send()

        @pl.loop(0, micro)
        def _(j):
            which = order_ref[0, j]
            s0 = start_ref[0, which]
            s1 = s0 + len_ref[0, which]
            here_rows = slice(0, seq)
            square = jnp.zeros((seq, 1), jnp.float32)
            for c in range(chunks):
                span = slice(c * width, (c + 1) * width)
                hop(j, c).wait_recv()
                wide = xin[j, c].astype(jnp.float32)
                square = square + jnp.sum(wide * wide, axis=-1, keepdims=True)
                scaled = (wide * gain_ref[:, span]).astype(jnp.bfloat16)

                @pl.loop(0, WIDE)
                def _(n):
                    cols = pl.ds(pl.multiple_of(n * (total // WIDE), total // WIDE), total // WIDE)
                    part = jnp.dot(scaled, wbuf[span, cols], preferred_element_type=jnp.float32)
                    if c == 0:
                        acc[here_rows, cols] = part
                    else:
                        acc[here_rows, cols] += part

            scale = lax.rsqrt(square * (1.0 / model) + EPS)

            for part, gains in ((0, qg_ref), (1, kg_ref)):
                factor = HEAD_DIM ** (-0.5) * LOG2_E if part == 0 else 1.0

                @pl.loop(0, model // (NORMS_AT_ONCE * HEAD_DIM))
                def _(n):
                    for i in range(NORMS_AT_ONCE):
                        base = (n * NORMS_AT_ONCE + i) * HEAD_DIM
                        here = pl.ds(pl.multiple_of(base, HEAD_DIM), HEAD_DIM)
                        cols = pl.ds(pl.multiple_of(part * model + base, HEAD_DIM), HEAD_DIM)
                        qkv[:, cols] = lifted_norm(acc[here_rows, cols], scale, gains[:, here] * factor)

            allowed = mask(s0, s1)

            @pl.loop(0, model // (HEADS_AT_ONCE * HEAD_DIM))
            def _(n):
                for i in range(HEADS_AT_ONCE):
                    base = (n * HEADS_AT_ONCE + i) * HEAD_DIM
                    here = pl.ds(pl.multiple_of(base, HEAD_DIM), HEAD_DIM)
                    q = qkv[:, here]
                    k = qkv[:, pl.ds(pl.multiple_of(model + base, HEAD_DIM), HEAD_DIM)]
                    v = acc[here_rows, pl.ds(pl.multiple_of(2 * model + base, HEAD_DIM), HEAD_DIM)] * scale
                    att[j, :, here] = head(q, k, v, allowed)

            leave(j)

    @pl.when(sec < sections - 1)
    def _():
        for j in range(micro):
            for c in range(chunks):
                hop(j, c).wait_send()


def solution(mesh):
    sections, devices = mesh.shape["section"], mesh.shape["dp"]

    def body(inputs, order, image_start, image_len, norm_gain, qkv_weight, q_gain, k_gain, o_weight):
        micro = order.shape[1]
        count, model = inputs.shape
        seq = count // micro
        total = qkv_weight.shape[2]
        shard = qkv_weight.shape[1]
        width = model // CHUNKS
        chunks = model // width
        chips = devices // 2
        length = chips // 2
        smem = pl.BlockSpec(memory_space=pltpu.SMEM)
        vmem = pl.BlockSpec(memory_space=pltpu.VMEM)
        hbm = pl.BlockSpec(memory_space=pltpu.HBM)
        dma = pltpu.SemaphoreType.DMA
        out = pl.pallas_call(
            functools.partial(kernel, sections, devices),
            out_shape=jax.ShapeDtypeStruct((micro, seq, model), jnp.bfloat16),
            in_specs=[smem, smem, smem, vmem, vmem, hbm, vmem, vmem, hbm],
            out_specs=vmem,
            scratch_shapes=[
                pltpu.VMEM((model, total), jnp.bfloat16),
                pltpu.VMEM((model, model), jnp.bfloat16),
                pltpu.VMEM((micro, chunks, seq, width), jnp.bfloat16),
                pltpu.VMEM((micro, chunks, seq, width), jnp.bfloat16),
                pltpu.VMEM((2 * seq, total), jnp.float32),
                pltpu.VMEM((seq, 2 * model), jnp.bfloat16),
                pltpu.VMEM((micro, seq, model), jnp.bfloat16),
                pltpu.VMEM((2, micro, chunks, seq, width), jnp.bfloat16),
                pltpu.VMEM((2, micro, seq, model // 4), jnp.bfloat16),
                pltpu.VMEM((3, seq, 128), jnp.float32),
                pltpu.VMEM((micro, 2, 8, 128), jnp.int32),
                pltpu.VMEM((2, micro, 2, 8, 128), jnp.int32),
                dma, dma, dma, dma,
                dma((2, SUBS, chips - 1)),
                dma((2, SUBS, chips - 1)),
                dma((2, SUBS, chips - 1)),
                dma((2, SUBS, chips - 1)),
                dma((micro, chunks)),
                dma((micro, chunks)),
                dma((2, PARTS)),
                dma((2, PARTS)),
                dma((2, PARTS)),
                dma((2, length - 1, 2, PARTS)),
                dma((2, length - 1, 2, PARTS)),
                dma((2, 2 * length - 1, PARTS)),
                dma((2, 2 * length - 1, PARTS)),
                dma((2, PARTS)),
                dma((2, PARTS)),
                dma((2, micro, chunks)),
                dma((2, micro, chunks)),
                dma((2, micro)),
                dma((2, micro)),
                dma((2,)),
                dma((2,)),
            ],
            compiler_params=pltpu.CompilerParams(
                collective_id=0, has_side_effects=True, vmem_limit_bytes=60 * 1024 * 1024
            ),
        )(
            order, image_start, image_len, inputs.reshape(micro, seq, model), norm_gain,
            qkv_weight.reshape(shard, total), q_gain, k_gain, o_weight.reshape(model, model),
        )
        return out.reshape(1, count, model)

    in_specs = (
        P("dp", None),
        P("dp", None),
        P("dp", None),
        P("dp", None),
        P("section", None),
        P("section", "dp", None),
        P("section", None),
        P("section", None),
        P("section", None, None),
    )
    out_specs = P("section", "dp", None)
    return jax.shard_map(body, mesh=mesh, in_specs=in_specs, out_specs=out_specs, check_vma=False)
```

time: 183 us -> 159 us (0.87)
  Pallas kernels: 181 us -> 156 us
    pallas_call x1, Pallas kernels: 181 us -> 156 us  [body(): pl.pallas_call(functools.partial(kernel, sections, devices), out_shape=ja...]
where the time goes in v1:
time: 159 us; the launch traced here: 158 us
  Pallas kernels  156 us (98%)
  local copies, waits for them, and re-layouts  2.3 us (1%)
    pallas_call x1, Pallas kernels, body(): pl.pallas_call(functools.partial(kernel, sections, devices), out_shape=ja...  156 us

profile of v1, /device:TPU:24, one launch (start us, length us, event | category | flops | bytes accessed | tf_op | source)
XLA Modules:
  0.0 158.4 jit_solution(14943534622722161206)
XLA Ops:
  0.0 156.1 %shard_map.91 = bf16[2,128,2048]{2,1,0:T(8,128)(2,1)} custom-call(s32[1,2]{1,0:T(1,128)} %order_ref.1, s32[1,2]{1,0:T(1,128)} %start_ref.1, s32[1,2]{1,0:T(1,128)} %len_ref.1, bf16[2,128,2048]{2,1,0:T(8,128)(2,1)} %bitcast.7, f32[1,2048]{1,0:T(1,128)} %gain_ref.1, bf16[256,6144]{1,0:T(8,128)(2,1)} %bitcast.6, f32[1,2048]{1,0:T(1,128)} %qg_ref.1, ...), custom_call_target="tpu_custom_call" | custom-call | tf_op jit(solution)/shard_map/pallas_call | solution.py:578
  156.1 2.3 %copy.11 = bf16[1,256,2048]{2,1,0:T(8,128)(2,1)} copy(bf16[1,256,2048]{2,1,0:T(8,128)(2,1)} %bitcast.5) | data formatting | bytes 2097152

commit v2 on v1

--- a/solution.py
+++ b/solution.py
@@ -10,12 +10,15 @@
 EPS = 1e-05
 LOG2_E = 1.4426950408889634
 SUBS = 2
-CHUNKS = 4
-WIDE = 1
+CHUNKS = 8
+GROUP = 2
+LAG = 3
+EARLY = ((2, 2, 1, 1), (0, 2, 1, 1))
 HEADS_AT_ONCE = 16
 NORMS_AT_ONCE = 16
-SHARED_SECTIONS = 2
+SHARED_SECTIONS = 3
 PARTS = 3
+RETURNS = 2
 MESH = pl.DeviceIdType.MESH
 
 
@@ -55,11 +58,12 @@
     sections, devices,
     order_ref, start_ref, len_ref, x_ref, gain_ref, w_ref, qg_ref, kg_ref, o_ref,
     out_ref,
-    wbuf, obuf, xin, xout, acc, qkv, att, xmate, ret, ssq, spans, mate_spans,
+    wbuf, obuf, xin, xout, acc, qkv, att, xmate, relay, ret, ssq, spans, mate_spans,
     own_sem, o_sem, first_send, first_recv, ring_send, ring_recv, pair_send, pair_recv,
     hop_send, hop_recv,
     own_sems, swap_send, swap_recv, loop_send, loop_recv, core_send, core_recv,
     mine_send, mine_recv, x_send, x_recv, give_send, give_recv, span_send, span_recv,
+    pass_send, pass_recv, fall_send, out_sem,
 ):
     chips = devices // 2
     grid_rows, columns = grid_of(chips)
@@ -67,8 +71,8 @@
     inverse = [order.index(c) for c in range(chips)]
     shard, total = w_ref.shape
     piece = shard // (2 * SUBS)
-    micro, chunks, seq, width = xin.shape
-    model = chunks * width
+    micro, seq, model = xin.shape
+    chunks, width = CHUNKS, model // CHUNKS
     quarter = model // 4
     few = quarter // HEAD_DIM
     sec = lax.axis_index("section")
@@ -136,8 +140,11 @@
 
             @pl.when(sec == 0)
             def _():
-                for c in range(chunks):
-                    xin[j, c] = x_ref[which, :, c * width : (c + 1) * width]
+                xin[j] = x_ref[which]
+
+            @pl.when(sec == 1 + j)
+            def _():
+                xout[j] = x_ref[which]
 
     @pl.when(jnp.logical_not(shared))
     def _():
@@ -163,11 +170,21 @@
         pl.semaphore_signal(barrier, inc=1, device_id=(below, me), device_id_type=MESH)
 
     line = (sec > 0).astype(jnp.int32) + (sec < sections - 1).astype(jnp.int32)
+    for j in range(1, micro):
+        for here, there in ((0, 1 + j), (1 + j, 0)):
+            @pl.when(sec == here)
+            def _():
+                pl.semaphore_signal(barrier, inc=1, device_id=(there, me), device_id_type=MESH)
+
+            line = line + (sec == here).astype(jnp.int32)
     pl.semaphore_wait(barrier, len(near) + line)
+
+    def span_of(c):
+        return pl.ds(c * width, width)
 
     def hop(j, c):
         return pltpu.make_async_remote_copy(
-            src_ref=xout.at[j, c], dst_ref=xin.at[j, c],
+            src_ref=xout.at[j, :, span_of(c)], dst_ref=xin.at[j, :, span_of(c)],
             send_sem=hop_send.at[j, c], recv_sem=hop_recv.at[j, c],
             device_id=(above, me), device_id_type=MESH,
         )
@@ -180,17 +197,22 @@
             (row_id >= s0) & (row_id < s1) & (col_id >= s0) & (col_id < s1)
         )
 
+    def out(j, g):
+        here = (j, slice(None), pl.ds(g * width, GROUP * width))
+        return pltpu.make_async_copy(xout.at[here], out_ref.at[here], out_sem.at[j, g // GROUP])
+
     def leave(j):
-        for c in range(chunks):
-            span = slice(c * width, (c + 1) * width)
+        for g in range(0, chunks, GROUP):
+            span = slice(g * width, (g + GROUP) * width)
             grown = jnp.dot(att[j], obuf[:, span], preferred_element_type=jnp.float32)
-            fresh = (xin[j, c].astype(jnp.float32) + grown).astype(jnp.bfloat16)
-            xout[j, c] = fresh
-            out_ref[j, :, span] = fresh
+            fresh = (xin[j, :, span].astype(jnp.float32) + grown).astype(jnp.bfloat16)
+            xout[j, :, span] = fresh
+            out(j, g).start()
 
             @pl.when(sec < sections - 1)
             def _():
-                hop(j, c).start()
+                for c in range(g, g + GROUP):
+                    hop(j, c).start()
 
     def head(q, k, v, allowed):
         scores = lax.dot_general(
@@ -247,13 +269,30 @@
 
         def share(s, j, c):
             return remote(
-                xin.at[j, c], xmate.at[s, j, c], x_send.at[s, j, c], x_recv.at[s, j, c], mates[s]
-            )
-
-        def give(s, j):
+                xin.at[j, :, span_of(c)], xmate.at[s, j, :, span_of(c)],
+                x_send.at[s, j, c], x_recv.at[s, j, c], mates[s],
+            )
+
+        def hand_on(s, j, c):
             return remote(
-                ret.at[s, j], att.at[j, :, aligned(units[s] * quarter, quarter)],
-                give_send.at[s, j], give_recv.at[s, j], mates[s],
+                xout.at[j, :, span_of(c)], relay.at[s, j, :, span_of(c)],
+                pass_send.at[s, j, c], pass_recv.at[s, j, c], mates[s],
+            )
+
+        def fall(s, j, c):
+            return pltpu.make_async_remote_copy(
+                src_ref=relay.at[s, j, :, span_of(c)], dst_ref=xmate.at[s, j, :, span_of(c)],
+                send_sem=fall_send.at[s, j, c], recv_sem=x_recv.at[s, j, c],
+                device_id=(0, me), device_id_type=MESH,
+            )
+
+        lot = quarter // RETURNS
+
+        def give(s, j, n):
+            return remote(
+                ret.at[s, j, :, pl.ds(n * lot, lot)],
+                att.at[j, :, aligned(units[s] * quarter + n * lot, lot)],
+                give_send.at[s, j, n], give_recv.at[s, j, n], mates[s],
             )
 
         def tell(s):
@@ -265,11 +304,12 @@
         for s in range(2):
             tell(s).start()
 
-        @pl.when(sec == 0)
-        def _():
-            for c in range(chunks):
-                for s in range(2):
-                    share(s, 0, c).start()
+        for j in range(micro):
+            @pl.when(sec == 1 + j)
+            def _():
+                for c in range(chunks):
+                    for s in range(2):
+                        hand_on(s, j, c).start()
 
         for p, s in both:
             swap(s, p).start()
@@ -284,18 +324,11 @@
                 out = out + x[:, i * 128 : (i + 1) * 128]
             return out
 
-        def take(ref, j, start, size):
-            if isinstance(start, int):
-                return ref[j, start // width, :, start % width : start % width + size]
-            if size == width:
-                return ref[j, lax.div(start, width)]
-            return ref[j, lax.div(start, width), :, aligned(lax.rem(start, width), size)]
-
         def project(j, s, start, size, parts, fresh):
             here = aligned(start, size)
             gain = gain_ref[:, here]
-            ours = take(xin, j, start, size).astype(jnp.float32)
-            theirs = take(xmate.at[s], j, start, size).astype(jnp.float32)
+            ours = xin[j, :, here].astype(jnp.float32)
+            theirs = xmate[s, j, :, here].astype(jnp.float32)
             left = jnp.concatenate(
                 [(ours * gain).astype(jnp.bfloat16), (theirs * gain).astype(jnp.bfloat16)], axis=0
             )
@@ -316,63 +349,89 @@
 
         chip_rows = 2 * shard
 
+        def arrive(i, p):
+            for s in range(2):
+                if i == 0:
+                    swap(s, p).wait_recv()
+                    circle(s, 1, 1, p).start()
+                else:
+                    k, b = (i + 1) // 2, (i + 1) % 2
+                    circle(s, k, b, p).wait_recv()
+                    if k < length - 1:
+                        circle(s, k + 1, b, p).start()
+                hand(s, i, p).start()
+
+        def finish(i, p):
+            for s in range(2):
+                hand(s, i, p).wait_recv()
+
+            @pl.when(sec == 0)
+            def _():
+                for s in range(2):
+                    start = lax.div(owner_of(s, i), 2) * chip_rows
+                    project(0, s, start, chip_rows, (p,), False)
+
+        def drop(j):
+            @pl.when(sec == 1 + j)
+            def _():
+                for c in range(chunks):
+                    for s in range(2):
+                        hand_on(s, j, c).wait_recv()
+                        fall(s, j, c).start()
+
+        drop(0)
+        for p in range(PARTS):
+            arrive(0, p)
+        for p, s in both:
+            stay(s, p).wait()
+            mine(s, p).wait_recv()
+
         @pl.when(sec == 0)
         def _():
             for c in range(chunks):
                 for s in range(2):
                     share(s, 0, c).wait_recv()
-
-        for p, s in both:
-            stay(s, p).wait()
-            mine(s, p).wait_recv()
-
-        @pl.when(sec == 0)
-        def _():
             for s in range(2):
                 project(0, s, chip * chip_rows, chip_rows, range(PARTS), True)
 
-        for i in range(waves):
-            def finish(p):
-                for s in range(2):
-                    hand(s, i, p).wait_recv()
-
-                @pl.when(sec == 0)
-                def _():
+        for p in range(PARTS):
+            finish(0, p)
+        for j in range(1, micro):
+            drop(j)
+        for i in range(1, waves):
+            for p in range(PARTS):
+                arrive(i, p)
+                if p > 0:
+                    finish(i, p - 1)
+            finish(i, PARTS - 1)
+
+        for j in range(micro):
+            @pl.when(sec == 1 + j)
+            def _():
+                for c in range(chunks):
                     for s in range(2):
-                        start = lax.div(owner_of(s, i), 2) * chip_rows
-                        project(0, s, start, chip_rows, (p,), False)
-
-            for p in range(PARTS):
-                for s in range(2):
-                    if i == 0:
-                        swap(s, p).wait_recv()
-                        circle(s, 1, 1, p).start()
-                    else:
-                        k, b = (i + 1) // 2, (i + 1) % 2
-                        circle(s, k, b, p).wait_recv()
-                        if k < length - 1:
-                            circle(s, k + 1, b, p).start()
-                    hand(s, i, p).start()
-                if p > 0:
-                    finish(p - 1)
-            finish(PARTS - 1)
+                        hand_on(s, j, c).wait_send()
 
         for s in range(2):
             tell(s).wait_recv()
         o_copy.wait()
 
-        def attend(turn, region, unit, scale, allowed, ref, base):
+        def ready(turn, region, unit, scale, heads):
             rows = slice(region * seq, (region + 1) * seq)
             for part, gains in ((0, qg_ref), (1, kg_ref)):
                 factor = HEAD_DIM ** (-0.5) * LOG2_E if part == 0 else 1.0
-                for i in range(few):
+                for i in heads:
                     start = unit * quarter + i * HEAD_DIM
                     p = acc[rows, aligned(part * model + start, HEAD_DIM)]
                     spot = (turn * 2 + part) * quarter + i * HEAD_DIM
                     qkv[:, spot : spot + HEAD_DIM] = lifted_norm(
                         p, scale, gains[:, aligned(start, HEAD_DIM)] * factor
                     )
-            for i in range(few):
+
+        def attend(turn, region, unit, scale, allowed, heads, ref, base):
+            ready(turn, region, unit, scale, heads)
+            rows = slice(region * seq, (region + 1) * seq)
+            for i in heads:
                 spot = turn * 2 * quarter + i * HEAD_DIM
                 v = acc[rows, aligned(2 * model + unit * quarter + i * HEAD_DIM, HEAD_DIM)] * scale
                 ref[:, aligned(base + i * HEAD_DIM, HEAD_DIM)] = head(
@@ -380,50 +439,71 @@
                     qkv[:, spot + quarter : spot + quarter + HEAD_DIM], v, allowed,
                 )
 
+        def pass_on(j, c):
+            hop(j, c).wait_recv()
+            for s in range(2):
+                share(s, j, c).start()
+
         @pl.loop(0, micro)
         def _(j):
+            def ahead_of(n):
+                for where, counts in ((sec == 1, EARLY[0]), (sec > 1, EARLY[1])):
+                    if counts[n] > 0:
+                        @pl.when(where & (j < micro - 1))
+                        def _():
+                            for c in range(sum(counts[:n]), sum(counts[: n + 1])):
+                                pass_on(j + 1, c)
+
             @pl.when((sec > 0) | (j > 0))
             def _():
-                def finish(c):
+                def finish(g):
+                    for c in range(g, g + GROUP):
+                        for s in range(2):
+                            share(s, j, c).wait_recv()
                     for s in range(2):
-                        share(s, j, c).wait_recv()
-                    for s in range(2):
-                        project(j, s, c * width, width, range(PARTS), c == 0)
-
-                for c in range(chunks):
-                    @pl.when(sec > 0)
-                    def _():
-                        hop(j, c).wait_recv()
-                        for s in range(2):
-                            share(s, j, c).start()
-
-                    if c > 0:
-                        finish(c - 1)
-                finish(chunks - 1)
+                        project(j, s, g * width, GROUP * width, range(PARTS), g == 0)
+
+                for c in range(chunks + LAG):
+                    if c < chunks:
+                        late = ((sec == 1) & (c >= sum(EARLY[0]))) | ((sec > 1) & (c >= sum(EARLY[1])))
+
+                        @pl.when((sec > 0) & ((j == 0) | late))
+                        def _():
+                            pass_on(j, c)
+
+                    if c == chunks + LAG - 1:
+                        ahead_of(0)
+                    done = c - LAG + 1
+                    if done > 0 and done % GROUP == 0:
+                        finish(done - GROUP)
 
             def scale_of(k):
                 square = jnp.sum(ssq[k], axis=-1, keepdims=True)
                 return lax.rsqrt(square * (1.0 / model) + EPS)
 
-            for s in range(2):
-                allowed = mask(mate_spans[s, j, 0, 0:1, :], mate_spans[s, j, 1, 0:1, :])
-                attend(s, 1, units[s], scale_of(1 + s), allowed, ret.at[s, j], 0)
-                give(s, j).start()
-
-            @pl.when((sec == 0) & (j < micro - 1))
-            def _():
-                for c in range(chunks):
-                    for s in range(2):
-                        share(s, j + 1, c).start()
-
+            scales = [scale_of(1 + s) for s in range(2)]
+            open_to = [
+                mask(mate_spans[s, j, 0, 0:1, :], mate_spans[s, j, 1, 0:1, :]) for s in range(2)
+            ]
+            for n in range(RETURNS):
+                heads = range(n * few // RETURNS, (n + 1) * few // RETURNS)
+                for s in range(2):
+                    attend(s, 1, units[s], scales[s], open_to[s], heads, ret.at[s, j], 0)
+                for s in range(2):
+                    give(s, j, n).start()
+
+            ahead_of(1)
             which = order_ref[0, j]
             s0 = start_ref[0, which]
             allowed = mask(s0, s0 + len_ref[0, which])
             scale = scale_of(0)
             for s in range(2):
-                attend(2 + s, 0, units[s], scale, allowed, att.at[j], units[s] * quarter)
-            for s in range(2):
-                give(s, j).wait_recv()
+                attend(2 + s, 0, units[s], scale, allowed, range(few), att.at[j], units[s] * quarter)
+            ahead_of(2)
+            for n in range(RETURNS):
+                for s in range(2):
+                    give(s, j, n).wait_recv()
+            ahead_of(3)
             leave(j)
 
         for s in range(2):
@@ -437,9 +517,22 @@
                     for b in range(2):
                         circle(s, k, b, p).wait_send()
             for j in range(micro):
-                give(s, j).wait_send()
-                for c in range(chunks):
-                    share(s, j, c).wait_send()
+                for n in range(RETURNS):
+                    give(s, j, n).wait_send()
+
+        @pl.when(sec > 0)
+        def _():
+            for s in range(2):
+                for j in range(micro):
+                    for c in range(chunks):
+                        share(s, j, c).wait_send()
+
+        for j in range(micro):
+            @pl.when(sec == 1 + j)
+            def _():
+                for s in range(2):
+                    for c in range(chunks):
+                        fall(s, j, c).wait_send()
 
     @pl.when(jnp.logical_not(shared))
     def _():
@@ -508,21 +601,18 @@
             s1 = s0 + len_ref[0, which]
             here_rows = slice(0, seq)
             square = jnp.zeros((seq, 1), jnp.float32)
-            for c in range(chunks):
-                span = slice(c * width, (c + 1) * width)
-                hop(j, c).wait_recv()
-                wide = xin[j, c].astype(jnp.float32)
+            for g in range(0, chunks, GROUP):
+                span = slice(g * width, (g + GROUP) * width)
+                for c in range(g, g + GROUP):
+                    hop(j, c).wait_recv()
+                wide = xin[j, :, span].astype(jnp.float32)
                 square = square + jnp.sum(wide * wide, axis=-1, keepdims=True)
                 scaled = (wide * gain_ref[:, span]).astype(jnp.bfloat16)
-
-                @pl.loop(0, WIDE)
-                def _(n):
-                    cols = pl.ds(pl.multiple_of(n * (total // WIDE), total // WIDE), total // WIDE)
-                    part = jnp.dot(scaled, wbuf[span, cols], preferred_element_type=jnp.float32)
-                    if c == 0:
-                        acc[here_rows, cols] = part
-                    else:
-                        acc[here_rows, cols] += part
+                part = jnp.dot(scaled, wbuf[span, :], preferred_element_type=jnp.float32)
+                if g == 0:
+                    acc[here_rows, :] = part
+                else:
+                    acc[here_rows, :] += part
 
             scale = lax.rsqrt(square * (1.0 / model) + EPS)
 
@@ -551,6 +641,10 @@
 
             leave(j)
 
+    for j in range(micro):
+        for g in range(0, chunks, GROUP):
+            out(j, g).wait()
+
     @pl.when(sec < sections - 1)
     def _():
         for j in range(micro):
@@ -567,8 +661,7 @@
         seq = count // micro
         total = qkv_weight.shape[2]
         shard = qkv_weight.shape[1]
-        width = model // CHUNKS
-        chunks = model // width
+        chunks = CHUNKS
         chips = devices // 2
         length = chips // 2
         smem = pl.BlockSpec(memory_space=pltpu.SMEM)
@@ -579,16 +672,17 @@
             functools.partial(kernel, sections, devices),
             out_shape=jax.ShapeDtypeStruct((micro, seq, model), jnp.bfloat16),
             in_specs=[smem, smem, smem, vmem, vmem, hbm, vmem, vmem, hbm],
-            out_specs=vmem,
+            out_specs=hbm,
             scratch_shapes=[
                 pltpu.VMEM((model, total), jnp.bfloat16),
                 pltpu.VMEM((model, model), jnp.bfloat16),
-                pltpu.VMEM((micro, chunks, seq, width), jnp.bfloat16),
-                pltpu.VMEM((micro, chunks, seq, width), jnp.bfloat16),
+                pltpu.VMEM((micro, seq, model), jnp.bfloat16),
+                pltpu.VMEM((micro, seq, model), jnp.bfloat16),
                 pltpu.VMEM((2 * seq, total), jnp.float32),
                 pltpu.VMEM((seq, 2 * model), jnp.bfloat16),
                 pltpu.VMEM((micro, seq, model), jnp.bfloat16),
-                pltpu.VMEM((2, micro, chunks, seq, width), jnp.bfloat16),
+                pltpu.VMEM((2, micro, seq, model), jnp.bfloat16),
+                pltpu.VMEM((2, micro, seq, model), jnp.bfloat16),
                 pltpu.VMEM((2, micro, seq, model // 4), jnp.bfloat16),
                 pltpu.VMEM((3, seq, 128), jnp.float32),
                 pltpu.VMEM((micro, 2, 8, 128), jnp.int32),
@@ -611,10 +705,14 @@
                 dma((2, PARTS)),
                 dma((2, micro, chunks)),
                 dma((2, micro, chunks)),
-                dma((2, micro)),
-                dma((2, micro)),
+                dma((2, micro, RETURNS)),
+                dma((2, micro, RETURNS)),
                 dma((2,)),
                 dma((2,)),
+                dma((2, micro, CHUNKS)),
+                dma((2, micro, CHUNKS)),
+                dma((2, micro, CHUNKS)),
+                dma((micro, CHUNKS // GROUP)),
             ],
             compiler_params=pltpu.CompilerParams(
                 collective_id=0, has_side_effects=True, vmem_limit_bytes=60 * 1024 * 1024

time: 159 us -> 152 us (0.956)
  Pallas kernels: 156 us -> 149 us
    pallas_call x1, Pallas kernels: 156 us -> 149 us  [body(): pl.pallas_call(functools.partial(kernel, sections, devices), out_shape=ja...]
where the time goes in v2:
time: 152 us
  Pallas kernels  149 us (98%)
  local copies, waits for them, and re-layouts  2.3 us (2%)
    pallas_call x1, Pallas kernels, body(): pl.pallas_call(functools.partial(kernel, sections, devices), out_shape=ja...  149 us

profile of v2, /device:TPU:24, one launch (start us, length us, event | category | flops | bytes accessed | tf_op | source)
XLA Modules:
  0.0 151.8 jit_solution(8017585577119993284)
XLA Ops:
  0.0 149.4 %shard_map.91 = bf16[2,128,2048]{2,1,0:T(8,128)(2,1)} custom-call(s32[1,2]{1,0:T(1,128)} %order_ref.1, s32[1,2]{1,0:T(1,128)} %start_ref.1, s32[1,2]{1,0:T(1,128)} %len_ref.1, bf16[2,128,2048]{2,1,0:T(8,128)(2,1)} %bitcast.7, f32[1,2048]{1,0:T(1,128)} %gain_ref.1, bf16[256,6144]{1,0:T(8,128)(2,1)} %bitcast.6, f32[1,2048]{1,0:T(1,128)} %qg_ref.1, ...), custom_call_target="tpu_custom_call" | custom-call | tf_op jit(solution)/shard_map/pallas_call | solution.py:671
  149.5 2.3 %copy.11 = bf16[1,256,2048]{2,1,0:T(8,128)(2,1)} copy(bf16[1,256,2048]{2,1,0:T(8,128)(2,1)} %bitcast.5) | data formatting | bytes 2097152

commit v3 on v2

--- a/solution.py
+++ b/solution.py
@@ -12,8 +12,10 @@
 SUBS = 2
 CHUNKS = 8
 GROUP = 2
-LAG = 3
-EARLY = ((2, 2, 1, 1), (0, 2, 1, 1))
+LAG = 5
+EARLY = ((2, 2, 1, 1, 1), (0, 2, 1, 1, 1))
+CARRIER = 2
+CARRIED = 2
 HEADS_AT_ONCE = 16
 NORMS_AT_ONCE = 16
 SHARED_SECTIONS = 3
@@ -58,12 +60,13 @@
     sections, devices,
     order_ref, start_ref, len_ref, x_ref, gain_ref, w_ref, qg_ref, kg_ref, o_ref,
     out_ref,
-    wbuf, obuf, xin, xout, acc, qkv, att, xmate, relay, ret, ssq, spans, mate_spans,
+    wbuf, obuf, xin, xout, acc, qkv, att, xmate, relay, ret, ssq, spans, mate_spans, wup, wover,
     own_sem, o_sem, first_send, first_recv, ring_send, ring_recv, pair_send, pair_recv,
     hop_send, hop_recv,
     own_sems, swap_send, swap_recv, loop_send, loop_recv, core_send, core_recv,
     mine_send, mine_recv, x_send, x_recv, give_send, give_recv, span_send, span_recv,
     pass_send, pass_recv, fall_send, out_sem,
+    up_send, up_recv, over_send, over_recv, down_send,
 ):
     chips = devices // 2
     grid_rows, columns = grid_of(chips)
@@ -123,6 +126,28 @@
         where = cols_of(units[s], p)
         return pltpu.make_async_copy(w_ref.at[:, where], wbuf.at[block(me), where], own_sems.at[s, p])
 
+    relays = [3 - j for j in range(micro)]
+    edges = sorted({(0, r) for r in relays} | {(0, CARRIER), (CARRIER, 0)})
+    barrier = pltpu.get_barrier_semaphore()
+    near = [mates[0], mates[1], partner]
+    if chips > 4:
+        near += [ahead, behind]
+        for s in range(2):
+            near += [seat(s, 1, False), seat(s, -1, False)]
+    for other in near:
+        pl.semaphore_signal(barrier, inc=1, device_id=(sec, other), device_id_type=MESH)
+    line = (sec < sections - 1).astype(jnp.int32)
+    for source, target in edges:
+        @pl.when(sec == source)
+        def _():
+            pl.semaphore_signal(barrier, inc=1, device_id=(target, me), device_id_type=MESH)
+
+        line = line + (sec == target).astype(jnp.int32)
+
+    @pl.when(sec > 0)
+    def _():
+        pl.semaphore_signal(barrier, inc=1, device_id=(below, me), device_id_type=MESH)
+
     o_copy = pltpu.make_async_copy(o_ref, obuf, o_sem)
     own_rows = block(me)
     own = pltpu.make_async_copy(w_ref, wbuf.at[own_rows], own_sem)
@@ -142,9 +167,10 @@
             def _():
                 xin[j] = x_ref[which]
 
-            @pl.when(sec == 1 + j)
-            def _():
-                xout[j] = x_ref[which]
+    for j in range(micro):
+        @pl.when(sec == relays[j])
+        def _():
+            xout[j] = x_ref[order_ref[0, j]]
 
     @pl.when(jnp.logical_not(shared))
     def _():
@@ -152,31 +178,6 @@
 
     o_copy.start()
 
-    barrier = pltpu.get_barrier_semaphore()
-    near = [mates[0], mates[1], partner]
-    if chips > 4:
-        near += [ahead, behind]
-        for s in range(2):
-            near += [seat(s, 1, False), seat(s, -1, False)]
-    for other in near:
-        pl.semaphore_signal(barrier, inc=1, device_id=(sec, other), device_id_type=MESH)
-
-    @pl.when(sec < sections - 1)
-    def _():
-        pl.semaphore_signal(barrier, inc=1, device_id=(above, me), device_id_type=MESH)
-
-    @pl.when(sec > 0)
-    def _():
-        pl.semaphore_signal(barrier, inc=1, device_id=(below, me), device_id_type=MESH)
-
-    line = (sec > 0).astype(jnp.int32) + (sec < sections - 1).astype(jnp.int32)
-    for j in range(1, micro):
-        for here, there in ((0, 1 + j), (1 + j, 0)):
-            @pl.when(sec == here)
-            def _():
-                pl.semaphore_signal(barrier, inc=1, device_id=(there, me), device_id_type=MESH)
-
-            line = line + (sec == here).astype(jnp.int32)
     pl.semaphore_wait(barrier, len(near) + line)
 
     def span_of(c):
@@ -197,12 +198,52 @@
             (row_id >= s0) & (row_id < s1) & (col_id >= s0) & (col_id < s1)
         )
 
+    def remote(source, dest, sent, got, other, level=None):
+        return pltpu.make_async_remote_copy(
+            src_ref=source, dst_ref=dest, send_sem=sent, recv_sem=got,
+            device_id=(sec if level is None else level, other), device_id_type=MESH,
+        )
+
+    def hand_on(s, j, c):
+        return remote(
+            xout.at[j, :, span_of(c)], relay.at[s, j, :, span_of(c)],
+            pass_send.at[s, j, c], pass_recv.at[s, j, c], mates[s],
+        )
+
+    def fall(s, j, c):
+        return remote(
+            relay.at[s, j, :, span_of(c)], xmate.at[s, j, :, span_of(c)],
+            fall_send.at[s, j, c], x_recv.at[s, j, c], me, 0,
+        )
+
+    pieces = [(c, s) for c in range(chunks) for s in range(2)]
+
+    def lift(j):
+        @pl.when(sec == relays[j])
+        def _():
+            for c, s in pieces:
+                hand_on(s, j, c).start()
+
+    def drop(j):
+        @pl.when(sec == relays[j])
+        def _():
+            for c, s in pieces:
+                hand_on(s, j, c).wait_recv()
+                fall(s, j, c).start()
+            for c, s in pieces:
+                hand_on(s, j, c).wait_send()
+
+    low = [j for j in range(micro) if relays[j] < SHARED_SECTIONS]
+    high = [j for j in range(micro) if relays[j] >= SHARED_SECTIONS]
+
     def out(j, g):
         here = (j, slice(None), pl.ds(g * width, GROUP * width))
         return pltpu.make_async_copy(xout.at[here], out_ref.at[here], out_sem.at[j, g // GROUP])
 
-    def leave(j):
+    def leave(j, between=None):
         for g in range(0, chunks, GROUP):
+            if between is not None and g == chunks // 2:
+                between()
             span = slice(g * width, (g + GROUP) * width)
             grown = jnp.dot(att[j], obuf[:, span], preferred_element_type=jnp.float32)
             fresh = (xin[j, :, span].astype(jnp.float32) + grown).astype(jnp.bfloat16)
@@ -231,12 +272,6 @@
 
     @pl.when(shared)
     def _():
-        def remote(source, dest, sent, got, other):
-            return pltpu.make_async_remote_copy(
-                src_ref=source, dst_ref=dest, send_sem=sent, recv_sem=got,
-                device_id=(sec, other), device_id_type=MESH,
-            )
-
         def swap(s, p):
             where = cols_of(flip(units[s]), p)
             return remote(
@@ -273,19 +308,6 @@
                 x_send.at[s, j, c], x_recv.at[s, j, c], mates[s],
             )
 
-        def hand_on(s, j, c):
-            return remote(
-                xout.at[j, :, span_of(c)], relay.at[s, j, :, span_of(c)],
-                pass_send.at[s, j, c], pass_recv.at[s, j, c], mates[s],
-            )
-
-        def fall(s, j, c):
-            return pltpu.make_async_remote_copy(
-                src_ref=relay.at[s, j, :, span_of(c)], dst_ref=xmate.at[s, j, :, span_of(c)],
-                send_sem=fall_send.at[s, j, c], recv_sem=x_recv.at[s, j, c],
-                device_id=(0, me), device_id_type=MESH,
-            )
-
         lot = quarter // RETURNS
 
         def give(s, j, n):
@@ -304,19 +326,51 @@
         for s in range(2):
             tell(s).start()
 
-        for j in range(micro):
-            @pl.when(sec == 1 + j)
-            def _():
-                for c in range(chunks):
-                    for s in range(2):
-                        hand_on(s, j, c).start()
-
-        for p, s in both:
+        def climb(s):
+            return remote(
+                w_ref.at[:, cols_of(units[s], CARRIED)], wup.at[s],
+                up_send.at[s], up_recv.at[s], me, CARRIER,
+            )
+
+        def cross(s):
+            return remote(
+                wup.at[s], wover.at[s], over_send.at[s], over_recv.at[s], seat(s, 1, False)
+            )
+
+        def sink(s):
+            rows = block(seat(s, -1, False))
+            return remote(
+                wover.at[s], wbuf.at[rows, cols_of(units[s], CARRIED)],
+                down_send.at[s], loop_recv.at[s, 0, 0, CARRIED], me, 0,
+            )
+
+        @pl.when(sec == 0)
+        def _():
+            for s in range(2):
+                climb(s).start()
+
+        for p, s in both[:4]:
             swap(s, p).start()
         for p, s in both:
             mine(s, p).start()
+
+        @pl.when(sec == CARRIER)
+        def _():
+            for s in range(2):
+                climb(s).wait_recv()
+                cross(s).start()
+
+        for j in low:
+            lift(j)
+        for p, s in both[4:]:
+            swap(s, p).start()
         for p, s in both:
-            circle(s, 1, 0, p).start()
+            if p == CARRIED:
+                @pl.when(sec > 0)
+                def _():
+                    circle(s, 1, 0, p).start()
+            else:
+                circle(s, 1, 0, p).start()
 
         def fold(x):
             out = x[:, :128]
@@ -371,17 +425,18 @@
                     start = lax.div(owner_of(s, i), 2) * chip_rows
                     project(0, s, start, chip_rows, (p,), False)
 
-        def drop(j):
-            @pl.when(sec == 1 + j)
-            def _():
-                for c in range(chunks):
-                    for s in range(2):
-                        hand_on(s, j, c).wait_recv()
-                        fall(s, j, c).start()
-
-        drop(0)
-        for p in range(PARTS):
+        for p in range(PARTS - 1):
             arrive(0, p)
+
+        @pl.when(sec == CARRIER)
+        def _():
+            for s in range(2):
+                cross(s).wait_recv()
+                sink(s).start()
+
+        for j in low:
+            drop(j)
+        arrive(0, PARTS - 1)
         for p, s in both:
             stay(s, p).wait()
             mine(s, p).wait_recv()
@@ -396,21 +451,12 @@
 
         for p in range(PARTS):
             finish(0, p)
-        for j in range(1, micro):
-            drop(j)
         for i in range(1, waves):
             for p in range(PARTS):
                 arrive(i, p)
                 if p > 0:
                     finish(i, p - 1)
             finish(i, PARTS - 1)
-
-        for j in range(micro):
-            @pl.when(sec == 1 + j)
-            def _():
-                for c in range(chunks):
-                    for s in range(2):
-                        hand_on(s, j, c).wait_send()
 
         for s in range(2):
             tell(s).wait_recv()
@@ -504,7 +550,7 @@
                 for s in range(2):
                     give(s, j, n).wait_recv()
             ahead_of(3)
-            leave(j)
+            leave(j, lambda: ahead_of(4))
 
         for s in range(2):
             tell(s).wait_send()
@@ -515,7 +561,8 @@
                     hand(s, i, p).wait_send()
                 for k in range(1, length):
                     for b in range(2):
-                        circle(s, k, b, p).wait_send()
+                        if (k, b, p) != (1, 0, CARRIED):
+                            circle(s, k, b, p).wait_send()
             for j in range(micro):
                 for n in range(RETURNS):
                     give(s, j, n).wait_send()
@@ -523,16 +570,21 @@
         @pl.when(sec > 0)
         def _():
             for s in range(2):
+                circle(s, 1, 0, CARRIED).wait_send()
                 for j in range(micro):
                     for c in range(chunks):
                         share(s, j, c).wait_send()
 
-        for j in range(micro):
-            @pl.when(sec == 1 + j)
-            def _():
-                for s in range(2):
-                    for c in range(chunks):
-                        fall(s, j, c).wait_send()
+        @pl.when(sec == 0)
+        def _():
+            for s in range(2):
+                climb(s).wait_send()
+
+        @pl.when(sec == CARRIER)
+        def _():
+            for s in range(2):
+                cross(s).wait_send()
+                sink(s).wait_send()
 
     @pl.when(jnp.logical_not(shared))
     def _():
@@ -561,6 +613,8 @@
                 device_id=(sec, partner), device_id_type=MESH,
             )
 
+        for j in high:
+            lift(j)
         ring = {}
         pair = {}
         for sub in range(SUBS):
@@ -572,6 +626,8 @@
             device_id=(sec, partner), device_id_type=MESH,
         )
         first.start()
+        for j in high:
+            drop(j)
         own.wait()
         first.wait_recv()
         for step in range(1, chips):
@@ -644,6 +700,11 @@
     for j in range(micro):
         for g in range(0, chunks, GROUP):
             out(j, g).wait()
+
+        @pl.when(sec == relays[j])
+        def _():
+            for c, s in pieces:
+                fall(s, j, c).wait_send()
 
     @pl.when(sec < sections - 1)
     def _():
@@ -687,6 +748,8 @@
                 pltpu.VMEM((3, seq, 128), jnp.float32),
                 pltpu.VMEM((micro, 2, 8, 128), jnp.int32),
                 pltpu.VMEM((2, micro, 2, 8, 128), jnp.int32),
+                pltpu.VMEM((2, shard, model // 4), jnp.bfloat16),
+                pltpu.VMEM((2, shard, model // 4), jnp.bfloat16),
                 dma, dma, dma, dma,
                 dma((2, SUBS, chips - 1)),
                 dma((2, SUBS, chips - 1)),
@@ -713,6 +776,11 @@
                 dma((2, micro, CHUNKS)),
                 dma((2, micro, CHUNKS)),
                 dma((micro, CHUNKS // GROUP)),
+                dma((2,)),
+                dma((2,)),
+                dma((2,)),
+                dma((2,)),
+                dma((2,)),
             ],
             compiler_params=pltpu.CompilerParams(
                 collective_id=0, has_side_effects=True, vmem_limit_bytes=60 * 1024 * 1024

time: 152 us -> 144 us (0.947)
  Pallas kernels: 149 us -> 141 us
    pallas_call x1, Pallas kernels: 149 us -> 141 us  [body(): pl.pallas_call(functools.partial(kernel, sections, devices), out_shape=ja...]
where the time goes in v3:
time: 144 us; the launch traced here: 143 us
  Pallas kernels  141 us (98%)
  local copies, waits for them, and re-layouts  2.3 us (2%)
    pallas_call x1, Pallas kernels, body(): pl.pallas_call(functools.partial(kernel, sections, devices), out_shape=ja...  141 us

profile of v3, /device:TPU:24, one launch (start us, length us, event | category | flops | bytes accessed | tf_op | source)
XLA Modules:
  0.0 143.0 jit_solution(3252093580059093472)
XLA Ops:
  0.0 140.7 %shard_map.91 = bf16[2,128,2048]{2,1,0:T(8,128)(2,1)} custom-call(s32[1,2]{1,0:T(1,128)} %order_ref.1, s32[1,2]{1,0:T(1,128)} %start_ref.1, s32[1,2]{1,0:T(1,128)} %len_ref.1, bf16[2,128,2048]{2,1,0:T(8,128)(2,1)} %bitcast.7, f32[1,2048]{1,0:T(1,128)} %gain_ref.1, bf16[256,6144]{1,0:T(8,128)(2,1)} %bitcast.6, f32[1,2048]{1,0:T(1,128)} %qg_ref.1, ...), custom_call_target="tpu_custom_call" | custom-call | tf_op jit(solution)/shard_map/pallas_call | solution.py:732
  140.7 2.3 %copy.11 = bf16[1,256,2048]{2,1,0:T(8,128)(2,1)} copy(bf16[1,256,2048]{2,1,0:T(8,128)(2,1)} %bitcast.5) | data formatting | bytes 2097152

commit v4 on v3

--- a/solution.py
+++ b/solution.py
@@ -11,7 +11,8 @@
 LOG2_E = 1.4426950408889634
 SUBS = 2
 CHUNKS = 8
-GROUP = 2
+GROUPS = (2, 2, 2, 2)
+EXITS = (2, 2, 2, 2)
 LAG = 5
 EARLY = ((2, 2, 1, 1, 1), (0, 2, 1, 1, 1))
 CARRIER = 2
@@ -52,13 +53,17 @@
     return value + 1 - 2 * lax.rem(value, 2)
 
 
+def runs(sizes):
+    return [(sum(sizes[:n]), size) for n, size in enumerate(sizes)]
+
+
 def aligned(start, size):
     return pl.ds(start if isinstance(start, int) else pl.multiple_of(start, size), size)
 
 
 def kernel(
     sections, devices,
-    order_ref, start_ref, len_ref, x_ref, gain_ref, w_ref, qg_ref, kg_ref, o_ref,
+    order_ref, start_ref, len_ref, x_hbm, gain_ref, w_ref, qg_ref, kg_ref, o_ref,
     out_ref,
     wbuf, obuf, xin, xout, acc, qkv, att, xmate, relay, ret, ssq, spans, mate_spans, wup, wover,
     own_sem, o_sem, first_send, first_recv, ring_send, ring_recv, pair_send, pair_recv,
@@ -66,7 +71,7 @@
     own_sems, swap_send, swap_recv, loop_send, loop_recv, core_send, core_recv,
     mine_send, mine_recv, x_send, x_recv, give_send, give_recv, span_send, span_recv,
     pass_send, pass_recv, fall_send, out_sem,
-    up_send, up_recv, over_send, over_recv, down_send,
+    up_send, up_recv, over_send, over_recv, down_send, x_ref, x_sem,
 ):
     chips = devices // 2
     grid_rows, columns = grid_of(chips)
@@ -128,6 +133,8 @@
 
     relays = [3 - j for j in range(micro)]
     edges = sorted({(0, r) for r in relays} | {(0, CARRIER), (CARRIER, 0)})
+    x_copy = pltpu.make_async_copy(x_hbm, x_ref, x_sem)
+    x_copy.start()
     barrier = pltpu.get_barrier_semaphore()
     near = [mates[0], mates[1], partner]
     if chips > 4:
@@ -157,6 +164,11 @@
         for s in range(2):
             for p in range(PARTS):
                 stay(s, p).start()
+
+    x_copy.wait()
+
+    @pl.when(shared)
+    def _():
         for j in range(micro):
             which = order_ref[0, j]
             s0 = start_ref[0, which]
@@ -237,22 +249,23 @@
     high = [j for j in range(micro) if relays[j] >= SHARED_SECTIONS]
 
     def out(j, g):
-        here = (j, slice(None), pl.ds(g * width, GROUP * width))
-        return pltpu.make_async_copy(xout.at[here], out_ref.at[here], out_sem.at[j, g // GROUP])
+        first, size = runs(EXITS)[g]
+        here = (j, slice(None), pl.ds(first * width, size * width))
+        return pltpu.make_async_copy(xout.at[here], out_ref.at[here], out_sem.at[j, g])
 
     def leave(j, between=None):
-        for g in range(0, chunks, GROUP):
-            if between is not None and g == chunks // 2:
+        for g, (first, size) in enumerate(runs(EXITS)):
+            if between is not None and 2 * first == chunks:
                 between()
-            span = slice(g * width, (g + GROUP) * width)
+            span = slice(first * width, (first + size) * width)
             grown = jnp.dot(att[j], obuf[:, span], preferred_element_type=jnp.float32)
             fresh = (xin[j, :, span].astype(jnp.float32) + grown).astype(jnp.bfloat16)
             xout[j, :, span] = fresh
-            out(j, g).start()
+            out_ref[j, :, span] = fresh
 
             @pl.when(sec < sections - 1)
             def _():
-                for c in range(g, g + GROUP):
+                for c in range(first, first + size):
                     hop(j, c).start()
 
     def head(q, k, v, allowed):
@@ -502,12 +515,12 @@
 
             @pl.when((sec > 0) | (j > 0))
             def _():
-                def finish(g):
-                    for c in range(g, g + GROUP):
+                def finish(first, size):
+                    for c in range(first, first + size):
                         for s in range(2):
                             share(s, j, c).wait_recv()
                     for s in range(2):
-                        project(j, s, g * width, GROUP * width, range(PARTS), g == 0)
+                        project(j, s, first * width, size * width, range(PARTS), first == 0)
 
                 for c in range(chunks + LAG):
                     if c < chunks:
@@ -519,9 +532,9 @@
 
                     if c == chunks + LAG - 1:
                         ahead_of(0)
-                    done = c - LAG + 1
-                    if done > 0 and done % GROUP == 0:
-                        finish(done - GROUP)
+                    for first, size in runs(GROUPS):
+                        if first + size == c - LAG + 1:
+                            finish(first, size)
 
             def scale_of(k):
                 square = jnp.sum(ssq[k], axis=-1, keepdims=True)
@@ -657,15 +670,15 @@
             s1 = s0 + len_ref[0, which]
             here_rows = slice(0, seq)
             square = jnp.zeros((seq, 1), jnp.float32)
-            for g in range(0, chunks, GROUP):
-                span = slice(g * width, (g + GROUP) * width)
-                for c in range(g, g + GROUP):
+            for first, size in runs(GROUPS):
+                span = slice(first * width, (first + size) * width)
+                for c in range(first, first + size):
                     hop(j, c).wait_recv()
                 wide = xin[j, :, span].astype(jnp.float32)
                 square = square + jnp.sum(wide * wide, axis=-1, keepdims=True)
                 scaled = (wide * gain_ref[:, span]).astype(jnp.bfloat16)
                 part = jnp.dot(scaled, wbuf[span, :], preferred_element_type=jnp.float32)
-                if g == 0:
+                if first == 0:
                     acc[here_rows, :] = part
                 else:
                     acc[here_rows, :] += part
@@ -698,9 +711,6 @@
             leave(j)
 
     for j in range(micro):
-        for g in range(0, chunks, GROUP):
-            out(j, g).wait()
-
         @pl.when(sec == relays[j])
         def _():
             for c, s in pieces:
@@ -731,9 +741,9 @@
         dma = pltpu.SemaphoreType.DMA
         out = pl.pallas_call(
             functools.partial(kernel, sections, devices),
-            out_shape=jax.ShapeDtypeStruct((micro, seq, model), jnp.bfloat16),
-            in_specs=[smem, smem, smem, vmem, vmem, hbm, vmem, vmem, hbm],
-            out_specs=hbm,
+            out_shape=pltpu.VMEM((micro, seq, model), jnp.bfloat16),
+            in_specs=[smem, smem, smem, hbm, vmem, hbm, vmem, vmem, hbm],
+            out_specs=vmem,
             scratch_shapes=[
                 pltpu.VMEM((model, total), jnp.bfloat16),
                 pltpu.VMEM((model, model), jnp.bfloat16),
@@ -775,12 +785,14 @@
                 dma((2, micro, CHUNKS)),
                 dma((2, micro, CHUNKS)),
                 dma((2, micro, CHUNKS)),
-                dma((micro, CHUNKS // GROUP)),
+                dma((micro, len(EXITS))),
                 dma((2,)),
                 dma((2,)),
                 dma((2,)),
                 dma((2,)),
                 dma((2,)),
+                pltpu.VMEM((micro, seq, model), jnp.bfloat16),
+                dma,
             ],
             compiler_params=pltpu.CompilerParams(
                 collective_id=0, has_side_effects=True, vmem_limit_bytes=60 * 1024 * 1024

time: 144 us -> 142 us (0.986)
  no operation moved by 1% of the time
where the time goes in v4:
time: 142 us; the launch traced here: 141 us
  Pallas kernels  140 us (99%)
    pallas_call x1, Pallas kernels, body(): pl.pallas_call(functools.partial(kernel, sections, devices), out_shape=pl...  140 us

profile of v4, /device:TPU:24, one launch (start us, length us, event | category | flops | bytes accessed | tf_op | source)
XLA Modules:
  0.0 140.9 jit_solution(12179402650508847130)
XLA Ops:
  0.0 139.9 %shard_map.91 = bf16[2,128,2048]{2,1,0:T(8,128)(2,1)S(1)} custom-call(s32[1,2]{1,0:T(1,128)} %order_ref.1, s32[1,2]{1,0:T(1,128)} %start_ref.1, s32[1,2]{1,0:T(1,128)} %len_ref.1, bf16[2,128,2048]{2,1,0:T(8,128)(2,1)} %bitcast.7, f32[1,2048]{1,0:T(1,128)} %gain_ref.1, bf16[256,6144]{1,0:T(8,128)(2,1)} %bitcast.6, f32[1,2048]{1,0:T(1,128)} %qg_ref.1, ...), custom_call_target="tpu_custom_call" | custom-call | tf_op jit(solution)/shard_map/pallas_call | solution.py:742
  139.9 1.0 copy.11
